TPU v7x, 32 devices: a whole 2x2x4 slice. The times are simulated.
32 devices in a mesh: dp: 8 (over y, x, core), tensor: 4 (over z).
Axes of the slice: x: 2, y: 2, z: 4, core: 2. Of those that a mesh axis runs over, the one named last changes fastest.
Arguments:
- saved_input: bfloat16 [2048, 6144], P('dp', 'tensor'), may hold values from -6 to 6
- queries: bfloat16 [2048, 1024], P('dp', 'tensor'), may hold values from -8 to 8
- keys: bfloat16 [2048, 1024], P('dp', 'tensor'), may hold values from -8 to 8
- value_weight: bfloat16 [6144, 1024], P(None, 'tensor'), may hold values from -0.109375 to 0.109375
- grad_attended: bfloat16 [2048, 1024], P('dp', 'tensor'), may hold values from -6 to 6
Outputs:
- grad_input: bfloat16 [2048, 6144], P('dp', 'tensor')
- grad_value_weight: float32 [6144, 1024], P('dp', 'tensor')
- grad_queries: bfloat16 [2048, 1024], P('dp', 'tensor')
- grad_keys: bfloat16 [2048, 1024], P('dp', 'tensor')
All inputs are finite; a program needn't handle non-finite values.
Results may differ from a plain program's by a relative error of at most 0.02.
Values may be sent and summed in bfloat16 or wider, within the bound.
A program may use at most 64 MiB of HBM per device.

v0:
```python
import functools

import jax
import jax.numpy as jnp
from jax import lax
from jax.experimental import pallas as pl
from jax.experimental.pallas import tpu as pltpu
from jax.sharding import PartitionSpec as P

HD = 128


def fused_kernel(
    n, chips,
    x, queries, keys, w, ga,
    gi, gw, gq, gk,
    wown, wfull, gvall, xpart, xt, qsend, rsrecv, vsend, vrecv, zsend, zrecv, fin, probs,
    send_sem, recv_sem, own_sem, fin_send, fin_recv,
):
    f32, bf16 = jnp.float32, jnp.bfloat16
    tokens, feat = x.shape
    width = w.shape[1]
    half = feat // 2
    wrows = feat // (2 * chips)
    prows = half // chips
    t = lax.axis_index("tensor")
    d = lax.axis_index("dp")
    c = d // 2
    k = d % 2
    scale = 1.0 / (HD ** 0.5)

    def level(o):
        return (d, lax.rem(t + o, n))

    def below(o):
        return (d, lax.rem(t + n - o, n))

    def chip(q):
        return (2 * lax.rem(c + q, chips) + k, t)

    partner = (2 * c + 1 - k, t)
    count = [0]
    started = []

    def copy(src, dst, device):
        i = count[0]
        count[0] += 1
        return pltpu.make_async_remote_copy(
            src_ref=src, dst_ref=dst, send_sem=send_sem.at[i], recv_sem=recv_sem.at[i],
            device_id=device, device_id_type=pl.DeviceIdType.MESH,
        )

    def go(cp):
        cp.start()
        started.append(cp)

    def rows(i, size):
        return pl.ds(pl.multiple_of(i * size, size), size)

    barrier = pltpu.get_barrier_semaphore()
    peers = [level(o) for o in range(1, n)] + [chip(q) for q in range(1, chips)] + [partner]
    for peer in peers:
        pl.semaphore_signal(
            barrier, inc=1, device_id=peer, device_id_type=pl.DeviceIdType.MESH
        )
    pl.semaphore_wait(barrier, len(peers))

    wz = {}

    def send_weight(o):
        first = lax.rem(t + o, n) * feat + d * wrows
        wz[o] = copy(
            w.at[pl.ds(pl.multiple_of(first, wrows), wrows)],
            wfull.at[o - 1, rows(d, wrows)],
            level(o),
        )
        go(wz[o])

    early = list(range(1, n))
    late = [o for o in range(1, n) if o not in early]
    for o in early:
        send_weight(o)
    own = rows(t, feat)
    own_copy = pltpu.make_async_copy(w.at[own], wown, own_sem.at[0])
    xcp = copy(
        x.at[:, pl.ds(pl.multiple_of((1 - k) * half, half), half)], xpart, partner
    )
    go(xcp)
    own_copy.start()

    row = lax.broadcasted_iota(jnp.int32, (tokens, tokens), 0)
    col = lax.broadcasted_iota(jnp.int32, (tokens, tokens), 1)
    causal = row >= col
    heads = width // HD
    for h in range(heads):
        cols = slice(h * HD, (h + 1) * HD)
        scores = lax.dot_general(
            queries[:, cols], keys[:, cols], (((1,), (1,)), ((), ())),
            preferred_element_type=f32,
        ) * scale
        scores = jnp.where(causal, scores, -jnp.inf)
        e = jnp.exp(scores - jnp.max(scores, axis=-1, keepdims=True))
        p = e / jnp.sum(e, axis=-1, keepdims=True)
        probs[h] = p
        gvall[0, 0:tokens, cols] = lax.dot_general(
            p.astype(bf16), ga[:, cols], (((0,), (0,)), ((), ())),
            preferred_element_type=f32,
        ).astype(bf16)

    gz, gd = {}, {}
    for o in range(1, n):
        gz[o] = copy(gvall.at[0, 0:tokens], gvall.at[o, 0:tokens], level(o))
        go(gz[o])
    gd[0] = copy(gvall.at[0, 0:tokens], gvall.at[0, tokens:2 * tokens], partner)
    go(gd[0])

    for o in late:
        send_weight(o)

    xt[:, 0:tokens] = x[:, pl.ds(pl.multiple_of(k * half, half), half)].T
    xcp.wait_recv()
    xt[:, tokens:2 * tokens] = xpart[...].T

    rs = {}

    def weight_term(o):
        gd[o].wait_recv()
        qsend[o] = jnp.dot(xt[...], gvall[o], preferred_element_type=f32).astype(bf16)
        for q in range(1, chips):
            rs[o, q] = copy(
                qsend.at[o, rows(lax.rem(c + q, chips), prows)], rsrecv.at[q - 1, o], chip(q)
            )
            go(rs[o, q])

    weight_term(0)

    wp, wd = {}, {}
    for o in early + late:
        wz[o].wait_recv()
        mine = wfull.at[o - 1, rows(d, wrows)]
        for q in range(1, chips):
            wp[o, q] = copy(mine, mine, chip(q))
            go(wp[o, q])
        wd[o, 0] = copy(mine, mine, partner)
        go(wd[o, 0])

    for o in range(1, n):
        gz[o].wait_recv()
        gd[o] = copy(
            gvall.at[o, 0:tokens], gvall.at[o, tokens:2 * tokens], partner
        )
        go(gd[o])
    for o in range(1, n):
        weight_term(o)

    for o in range(1, n):
        for q in range(1, chips):
            wp[o, q].wait_recv()
            theirs = wfull.at[o - 1, rows(2 * lax.rem(c + chips - q, chips) + k, wrows)]
            wd[o, q] = copy(theirs, theirs, partner)
            go(wd[o, q])
    vz = {}
    for o in range(1, n):
        for q in range(chips):
            wd[o, q].wait_recv()
        vsend[o - 1] = jnp.dot(
            x[...], wfull[o - 1], preferred_element_type=f32
        ).astype(bf16)
        vz[o] = copy(vsend.at[o - 1], vrecv.at[o - 1], below(o))
        go(vz[o])

    az = {}
    for o in range(n):
        total = qsend[o, rows(c, prows)].astype(f32)
        for q in range(1, chips):
            rs[o, q].wait_recv()
            total = total + rsrecv[q - 1, o].astype(f32)
        if o == 0:
            zrecv[0] = total.astype(bf16)
        else:
            zsend[o - 1] = total.astype(bf16)
            az[o] = copy(zsend.at[o - 1], zrecv.at[o], below(o))
            go(az[o])

    own_copy.wait()
    contract = (((1,), (1,)), ((), ()))
    acc = lax.dot_general(
        gvall[0, 0:tokens], wown[...], contract, preferred_element_type=f32
    )
    for o in range(1, n):
        acc = acc + lax.dot_general(
            gvall[o, 0:tokens], wfull[o - 1], contract, preferred_element_type=f32
        )
    gi[...] = acc.astype(bf16)

    def last(o, q):
        return pltpu.make_async_remote_copy(
            src_ref=zrecv.at[o], dst_ref=fin.at[c],
            send_sem=fin_send.at[q], recv_sem=fin_recv.at[q],
            device_id=(2 * lax.rem(c + q, chips) + k, t),
            device_id_type=pl.DeviceIdType.MESH,
        )

    groups = float(2 * chips)
    for o in range(n):
        if o > 0:
            az[o].wait_recv()
        block = lax.rem(t + o, n)

        @pl.when(block != c)
        def _():
            last(o, lax.rem(block + chips - c, chips)).start()

        @pl.when(block == c)
        def _():
            gw[rows(c, prows), :] = zrecv[o].astype(f32) / groups

    values = jnp.dot(x[...], wown[...], preferred_element_type=f32)
    for o in range(1, n):
        vz[o].wait_recv()
        values = values + vrecv[o - 1].astype(f32)
    values = values.astype(bf16)
    for h in range(heads):
        cols = slice(h * HD, (h + 1) * HD)
        grad_probs = lax.dot_general(
            ga[:, cols], values[:, cols], contract, preferred_element_type=f32
        )
        p = probs[h]
        row_dot = jnp.sum(p * grad_probs, axis=-1, keepdims=True)
        gs = (p * (grad_probs - row_dot) * scale).astype(bf16)
        gq[:, cols] = jnp.dot(gs, keys[:, cols], preferred_element_type=f32).astype(bf16)
        gk[:, cols] = lax.dot_general(
            gs, queries[:, cols], (((0,), (0,)), ((), ())), preferred_element_type=f32
        ).astype(bf16)

    for q in range(1, chips):
        last(0, q).wait_recv()
        theirs = lax.rem(c + chips - q, chips)
        gw[rows(theirs, prows), :] = fin[theirs].astype(f32) / groups
        last(0, q).wait_send()
    for cp in started:
        cp.wait_send()


def write_out(*refs):
    results, outs, sem = refs[:4], refs[4:8], refs[8]
    moves = [
        pltpu.make_async_copy(results[i], outs[i], sem.at[i]) for i in range(4)
    ]
    for move in moves:
        move.start()
    for move in moves:
        move.wait()


def fused(n, groups, saved_input, queries, keys, value_weight, grad_attended):
    chips = groups // 2
    tokens, feat = saved_input.shape
    depth, width = value_weight.shape
    half, prows = feat // 2, feat // groups
    bf16 = jnp.bfloat16
    levels = n - 1
    copies = (
        levels * (3 + chips - 1 + chips) + 1 + n + n * (chips - 1) + levels
    )
    vmem = pl.BlockSpec(memory_space=pltpu.VMEM)
    results = pl.pallas_call(
        functools.partial(fused_kernel, n, chips),
        out_shape=(
            pltpu.VMEM((tokens, feat), bf16),
            pltpu.VMEM((depth // groups, width), jnp.float32),
            pltpu.VMEM(queries.shape, bf16),
            pltpu.VMEM(keys.shape, bf16),
        ),
        in_specs=[vmem] * 3 + [pl.BlockSpec(memory_space=pl.ANY), vmem],
        out_specs=(vmem,) * 4,
        scratch_shapes=[
            pltpu.VMEM((feat, width), bf16),
            pltpu.VMEM((levels, feat, width), bf16),
            pltpu.VMEM((n, 2 * tokens, width), bf16),
            pltpu.VMEM((tokens, half), bf16),
            pltpu.VMEM((half, 2 * tokens), bf16),
            pltpu.VMEM((n, half, width), bf16),
            pltpu.VMEM((chips - 1, n, prows, width), bf16),
            pltpu.VMEM((levels, tokens, width), bf16),
            pltpu.VMEM((levels, tokens, width), bf16),
            pltpu.VMEM((levels, prows, width), bf16),
            pltpu.VMEM((n, prows, width), bf16),
            pltpu.VMEM((chips, prows, width), bf16),
            pltpu.VMEM((width // HD, tokens, tokens), jnp.float32),
            pltpu.SemaphoreType.DMA((copies,)),
            pltpu.SemaphoreType.DMA((copies,)),
            pltpu.SemaphoreType.DMA((1,)),
            pltpu.SemaphoreType.DMA((chips,)),
            pltpu.SemaphoreType.DMA((chips,)),
        ],
        compiler_params=pltpu.CompilerParams(
            collective_id=0, has_side_effects=True, vmem_limit_bytes=58 * 2**20
        ),
    )(saved_input, queries, keys, value_weight, grad_attended)
    return pl.pallas_call(
        write_out,
        out_shape=tuple(jax.ShapeDtypeStruct(r.shape, r.dtype) for r in results),
        in_specs=[vmem] * 4,
        out_specs=(pl.BlockSpec(memory_space=pl.ANY),) * 4,
        scratch_shapes=[pltpu.SemaphoreType.DMA((4,))],
        compiler_params=pltpu.CompilerParams(vmem_limit_bytes=8 * 2**20),
    )(*results)


def on_device(saved_input, queries, keys, value_weight, grad_attended):
    token_count = queries.shape[0]
    local_width = value_weight.shape[1]
    local_heads = local_width // HD
    score_scale = 1.0 / jnp.sqrt(jnp.float32(HD))
    full_input = lax.all_gather(saved_input, "tensor", axis=1, tiled=True)
    values = jnp.dot(full_input, value_weight, preferred_element_type=jnp.float32).astype(
        jnp.bfloat16
    )
    query_heads = queries.reshape(token_count, local_heads, HD)
    key_heads = keys.reshape(token_count, local_heads, HD)
    value_heads = values.reshape(token_count, local_heads, HD)
    grad_heads = grad_attended.reshape(token_count, local_heads, HD)
    scores = (
        jnp.einsum("qhd,khd->hqk", query_heads, key_heads, preferred_element_type=jnp.float32)
        * score_scale
    )
    positions = lax.iota(jnp.int32, token_count)
    causal = positions[:, None] >= positions[None, :]
    scores = jnp.where(causal[None], scores, -jnp.inf)
    row_max = jnp.max(scores, axis=-1, keepdims=True)
    weights_exp = jnp.exp(scores - row_max)
    attention = weights_exp / jnp.sum(weights_exp, axis=-1, keepdims=True)
    probs_half = attention.astype(jnp.bfloat16)
    grad_values = jnp.einsum(
        "hqk,qhd->khd", probs_half, grad_heads, preferred_element_type=jnp.float32
    ).astype(jnp.bfloat16)
    grad_probs = jnp.einsum(
        "qhd,khd->hqk", grad_heads, value_heads, preferred_element_type=jnp.float32
    )
    row_dot = jnp.sum(attention * grad_probs, axis=-1, keepdims=True)
    grad_scores = (attention * (grad_probs - row_dot) * score_scale).astype(jnp.bfloat16)
    grad_queries = jnp.einsum(
        "hqk,khd->qhd", grad_scores, key_heads, preferred_element_type=jnp.float32
    ).astype(jnp.bfloat16)
    grad_keys = jnp.einsum(
        "hqk,qhd->khd", grad_scores, query_heads, preferred_element_type=jnp.float32
    ).astype(jnp.bfloat16)
    value_flat = grad_values.reshape(token_count, local_width)
    data_groups = lax.axis_size("dp")
    partial_value = lax.dot_general(
        value_flat, value_weight, (((1,), (1,)), ((), ())), preferred_element_type=jnp.float32
    )
    grad_input = lax.psum_scatter(
        partial_value.astype(jnp.bfloat16), "tensor", scatter_dimension=1, tiled=True
    )
    partial_value = lax.dot_general(
        full_input, value_flat, (((0,), (0,)), ((), ())), preferred_element_type=jnp.float32
    )
    summed = lax.psum_scatter(
        partial_value.astype(jnp.bfloat16), "dp", scatter_dimension=0, tiled=True
    ).astype(jnp.float32)
    grad_value_weight = summed / jnp.float32(data_groups)
    return (
        grad_input,
        grad_value_weight,
        grad_queries.reshape(token_count, local_width),
        grad_keys.reshape(token_count, local_width),
    )


def solution(mesh):
    placed = (
        P("dp", "tensor"),
        P("dp", "tensor"),
        P("dp", "tensor"),
        P(None, "tensor"),
        P("dp", "tensor"),
    )
    levels, groups = mesh.shape["tensor"], mesh.shape["dp"]
    run = on_device
    if groups == 2 * levels and levels > 1:
        run = functools.partial(fused, levels, groups)
    return jax.shard_map(
        run,
        mesh=mesh,
        in_specs=placed,
        out_specs=(P("dp", "tensor"), P("dp", "tensor"), P("dp", "tensor"), P("dp", "tensor")),
        check_vma=False,
    )
```

profile of v0, /device:TPU:0, one launch (start us, length us, event | category | flops | bytes accessed | tf_op | source)
XLA Modules:
  0.0 57.9 jit_solution(14441454304201027110)
XLA Ops:
  0.6 56.0 %shard_map.84 = (bf16[256,1536]{1,0:T(8,128)(2,1)S(1)}, f32[768,256]{1,0:T(8,128)S(1)}, bf16[256,256]{1,0:T(8,128)(2,1)S(1)}, bf16[256,256]{1,0:T(8,128)(2,1)S(1)}) custom-call(bf16[256,1536]{1,0:T(8,128)(2,1)} %x.1, bf16[256,256]{1,0:T(8,128)(2,1)} %queries.1, bf16[256,256]{1,0:T(8,128)(2,1)} %keys.1, bf16[6144,256]{1,0:T(8,128)(2,1)} %w.1, bf16[256,256]{1,0:T(8,128)(2,1)} %ga.1), custom_call_target="tpu_custom_call" | custom-call | tf_op jit(solution)/shard_map/pallas_call | solution.py:267
  56.6 1.3 %shard_map.85 = (bf16[256,1536]{1,0:T(8,128)(2,1)}, f32[768,256]{1,0:T(8,128)}, bf16[256,256]{1,0:T(8,128)(2,1)}, bf16[256,256]{1,0:T(8,128)(2,1)}) custom-call(bf16[256,1536]{1,0:T(8,128)(2,1)S(1)} %get-tuple-element.8.refs_0_, f32[768,256]{1,0:T(8,128)S(1)} %get-tuple-element.9.refs_1_, bf16[256,256]{1,0:T(8,128)(2,1)S(1)} %get-tuple-element.10.refs_2_, ...), custom_call_target="tpu_custom_call" | custom-call | tf_op jit(solution)/shard_map/pallas_call | solution.py:301
where the time goes:
time: 58 us; the launch traced here: 57.9 us
  Pallas kernels  57.2 us (99%)
  between operations  0.64 us (1%)
    pallas_call x1, Pallas kernels, fused(): pl.pallas_call(functools.partial(fused_kernel, n, chips), out_shape=(pltp...  56 us
    pallas_call x1, Pallas kernels, fused(): pl.pallas_call(write_out, out_shape=tuple((jax.ShapeDtypeStruct(r.shape,...  1.25 us

commit v1 on v0

v1 whole, which is shorter than its diff:
```python
import functools
import math

import jax
import jax.numpy as jnp
from jax import lax
from jax.experimental import pallas as pl
from jax.experimental.pallas import tpu as pltpu
from jax.sharding import PartitionSpec as P

HD = 128


def fused_kernel(
    n, chips,
    x_hbm, q_hbm, k_hbm, w, ga_hbm,
    gi, gw, gq, gk,
    x, queries, keys, ga,
    wfull, gvall, xt, qs, r1x, r1y, t2, r2x, r2y, zs, fin,
    part, vsend, vrecv, vals, probs, wsend,
    send_sem, recv_sem, load_sem,
):
    f32, bf16 = jnp.float32, jnp.bfloat16
    tokens, width = queries.shape
    feat = x.shape[1]
    crows = feat // chips
    hr = crows // 2
    heads = width // HD
    t = lax.axis_index("tensor")
    d = lax.axis_index("dp")
    c, k = d // 2, d % 2
    cx, cy = c % 2, c // 2
    scale = 1.0 / (HD ** 0.5)
    last = n - 1
    upper = t // (n // 2)
    edge = (t % last) == 0
    mid = (t % last) != 0
    outer = jnp.where(edge, 1, 0)
    level = [t, t + 1 - 2 * (t % 2), last - last * upper, n // 2 - upper]

    def at(s):
        return (d, s)

    partner = (d + 1 - 2 * k, t)
    xn = (d + 2 - 4 * cx, t)
    yn = (d + 4 - 8 * cy, t)
    diagonal = (d + 2 - 4 * cx + 4 - 8 * cy, t)
    chip_x, chip_y, chip_d = c + 1 - 2 * cx, c + 2 - 4 * cy, last - c

    counts = [0, 0]
    pending = []

    def slot():
        counts[1] += 1
        return counts[1] - 1

    def slots():
        return [slot() for _ in range(n)]

    def copy(src, dst, device, recv, when=None):
        i = counts[0]
        counts[0] += 1
        cp = pltpu.make_async_remote_copy(
            src_ref=src, dst_ref=dst, send_sem=send_sem.at[i], recv_sem=recv_sem.at[recv],
            device_id=device, device_id_type=pl.DeviceIdType.MESH,
        )
        if when is None:
            cp.start()
        else:
            pl.when(when)(cp.start)
        pending.append((i, math.prod(src.shape) // width, when))

    def drain(sent):
        for i, size, when in sent:
            ref = wfull.at[0, 0:size]
            cp = pltpu.make_async_remote_copy(
                src_ref=ref, dst_ref=ref, send_sem=send_sem.at[i], recv_sem=recv_sem.at[0],
                device_id=partner, device_id_type=pl.DeviceIdType.MESH,
            )
            if when is None:
                cp.wait_send()
            else:
                pl.when(when)(cp.wait_send)

    def arrive(recv, ref):
        pltpu.make_async_remote_copy(
            src_ref=ref, dst_ref=ref, send_sem=send_sem.at[0], recv_sem=recv_sem.at[recv],
            device_id=partner, device_id_type=pl.DeviceIdType.MESH,
        ).wait_recv()

    def rows(i, size):
        return pl.ds(pl.multiple_of(i * size, size), size)

    mine, theirs = rows(k, tokens), rows(1 - k, tokens)

    barrier = pltpu.get_barrier_semaphore()
    peers = [at((t + o) % n) for o in range(1, n)] + [xn, yn, diagonal, partner]
    for peer in peers:
        pl.semaphore_signal(
            barrier, inc=1, device_id=peer, device_id_type=pl.DeviceIdType.MESH
        )
    loads = [
        pltpu.make_async_copy(src, dst, load_sem.at[i])
        for i, (src, dst) in enumerate([
            (q_hbm, queries), (k_hbm, keys), (ga_hbm, ga), (x_hbm, x.at[mine]),
            (w.at[rows(t, feat)], wfull.at[t]),
        ])
    ]
    for load in loads:
        load.start()
    ahead = [
        pltpu.make_async_copy(
            w.at[pl.ds(pl.multiple_of(level[i] * feat + c * crows, crows), crows)],
            wsend.at[i - 1], load_sem.at[4 + i],
        )
        for i in range(1, n)
    ]
    for load in ahead:
        load.start()
    for load in loads[:3]:
        load.wait()

    row = lax.broadcasted_iota(jnp.int32, (tokens, tokens), 0)
    col = lax.broadcasted_iota(jnp.int32, (tokens, tokens), 1)
    causal = row >= col
    for h in range(heads):
        cols = slice(h * HD, (h + 1) * HD)
        scores = lax.dot_general(
            queries[:, cols], keys[:, cols], (((1,), (1,)), ((), ())),
            preferred_element_type=f32,
        ) * scale
        scores = jnp.where(causal, scores, -jnp.inf)
        e = jnp.exp(scores - jnp.max(scores, axis=-1, keepdims=True))
        p = e / jnp.sum(e, axis=-1, keepdims=True)
        probs[h] = p
        gvall[t, mine, cols] = lax.dot_general(
            p.astype(bf16), ga[:, cols], (((0,), (0,)), ((), ())),
            preferred_element_type=f32,
        ).astype(bf16)
    for load in ahead:
        load.wait()
    loads[3].wait()
    pl.semaphore_wait(barrier, len(peers))

    xs, gvs, ws, vs = slot(), slots(), slots(), slot()
    gza, gzb = slots(), slots()
    wz, wpx, wpy, wqx, wqy, wrx, wry = (slots() for _ in range(7))
    p1x, p1y, p2x, p2y = slots(), slots(), slots(), slots()
    vz = slots()
    fs = [slot() for _ in range(chips // 2)]
    home = c == t
    here = jnp.logical_and(home, cy == 1)
    away = jnp.logical_not(here)
    contract = (((1,), (1,)), ((), ()))

    def grad_in():
        acc = lax.dot_general(
            gvall[t, mine, :], wfull[t], contract, preferred_element_type=f32
        )
        for i in range(1, n):
            acc = acc + lax.dot_general(
                gvall[level[i], mine, :], wfull[level[i]], contract,
                preferred_element_type=f32,
            )
        gi[...] = acc.astype(bf16)

    @pl.when(k == 0)
    def _():
        def chunk(i, who, first=0, size=crows):
            start = pl.multiple_of(who * crows, crows) + first
            return wfull.at[level[i], pl.ds(pl.multiple_of(start, hr), size)]

        for i in (2, 3, 1):
            copy(
                wsend.at[i - 1],
                wfull.at[t, rows(c, crows)],
                at(level[i]),
                wz[1] if i == 1 else wz[3] - outer,
            )
        copy(gvall.at[t, mine], gvall.at[t, mine], partner, gvs[0])
        copy(x.at[mine], x.at[mine], partner, xs)

        def spread(i):
            arrive(wz[i], chunk(i, c))
            low, high = chunk(i, c, 0, hr), chunk(i, c, hr, hr)
            copy(high, high, xn, wpx[i])
            copy(low, low, yn, wpy[i])
            copy(low, low, xn, wqx[i])
            copy(high, high, yn, wqy[i])

        def spread_on(i):
            piece = chunk(i, chip_x, hr, hr)
            arrive(wpx[i], piece)
            copy(piece, piece, yn, wry[i])
            piece = chunk(i, chip_y, 0, hr)
            arrive(wpy[i], piece)
            copy(piece, piece, xn, wrx[i])

        def spread_end(i):
            arrive(wqx[i], chunk(i, chip_x, 0, hr))
            arrive(wqy[i], chunk(i, chip_y, hr, hr))
            arrive(wrx[i], chunk(i, chip_d, 0, hr))
            arrive(wry[i], chunk(i, chip_d, hr, hr))
            copy(wfull.at[level[i]], wfull.at[level[i]], partner, ws[i])

        def value_part(i):
            part[i - 1] = jnp.dot(x[...], wfull[level[i]], preferred_element_type=f32)
            if i == 1:
                vsend[0] = part[0].astype(bf16)
                copy(vsend.at[0], vrecv.at[1], at(level[1]), vz[1])
            else:
                @pl.when(edge)
                def _():
                    vsend[i - 1] = part[i - 1].astype(bf16)
                copy(vsend.at[i - 1], vrecv.at[i], at(level[1]), vz[i], when=edge)

        def value_sum(i):
            @pl.when(mid)
            def _():
                arrive(vz[i], vrecv.at[i])
                vsend[i - 1] = (part[i - 1] + vrecv[i].astype(f32)).astype(bf16)
            copy(vsend.at[i - 1], vrecv.at[0], at(level[i]), vz[0], when=mid)

        spread(2)
        spread(1)
        spread_on(2)
        spread(3)
        spread_on(1)
        arrive(xs, x.at[theirs])
        spread_on(3)
        spread_end(2)
        value_part(2)
        spread_end(3)
        value_part(3)
        spread_end(1)
        value_part(1)
        value_sum(2)
        value_sum(3)
        loads[4].wait()
        part[0] = jnp.dot(x[...], wfull[t], preferred_element_type=f32)
        for i in range(1, n):
            arrive(gvs[i], gvall.at[level[i], mine])
        grad_in()
        arrive(vz[1], vrecv.at[1])
        arrive(vz[0], vrecv.at[0])
        vals[...] = (
            part[0] + vrecv[1].astype(f32) + vrecv[0].astype(f32)
        ).astype(bf16)
        copy(vals.at[theirs], vals.at[theirs], partner, vs)

    sent_w = list(pending)
    pending.clear()

    @pl.when(k == 1)
    def _():
        def gv(i, which):
            return gvall.at[level[i], which]

        def send_gv():
            for to, far in ((1, 0), (3, outer)):
                for which, got in ((mine, gza), (theirs, gzb)):
                    copy(gv(0, which), gv(0, which), at(level[to]), got[to] - far)

        copy(x.at[mine], x.at[mine], partner, xs)
        arrive(gvs[0], gv(0, theirs))

        def pass_on(i):
            @pl.when(mid)
            def _():
                arrive(gza[i], gv(i, mine))
            copy(gv(i, mine), gv(i, mine), at(level[1]), gza[i], when=mid)

            @pl.when(mid)
            def _():
                arrive(gzb[i], gv(i, theirs))
            copy(gv(i, theirs), gv(i, theirs), at(level[1]), gzb[i], when=mid)

        def pass_over(i):
            @pl.when(edge if i > 1 else t >= 0)
            def _():
                arrive(gza[i], gv(i, mine))
                arrive(gzb[i], gv(i, theirs))
            copy(gv(i, theirs), gv(i, theirs), partner, gvs[i])

        def weight_term(i):
            term = jnp.dot(xt[...], gvall[level[i]], preferred_element_type=f32).astype(bf16)
            for j in range(chips):
                qs[i, j // 2, j % 2] = term[j * crows:(j + 1) * crows]
            copy(qs.at[i, :, 1 - cx, 0:hr, :], r1x.at[i], xn, p1x[i])
            copy(qs.at[i, 1 - cy, :, hr:crows, :], r1y.at[i], yn, p1y[i])

        def second_phase(i):
            arrive(p1x[i], r1x.at[i])
            t2[i, 0] = (
                qs[i, 1 - cy, cx, 0:hr, :].astype(f32) + r1x[i, 1 - cy].astype(f32)
            ).astype(bf16)
            copy(t2.at[i, 0], r2y.at[i], yn, p2y[i])
            arrive(p1y[i], r1y.at[i])
            t2[i, 1] = (
                qs[i, cy, 1 - cx, hr:crows, :].astype(f32) + r1y[i, 1 - cx].astype(f32)
            ).astype(bf16)
            copy(t2.at[i, 1], r2x.at[i], xn, p2x[i])

        def finish(i):
            arrive(p2y[i], r2y.at[i])
            zs[i, 0:hr, :] = (
                qs[i, cy, cx, 0:hr, :].astype(f32) + r1x[i, cy].astype(f32)
                + r2y[i].astype(f32)
            ).astype(bf16)
            arrive(p2x[i], r2x.at[i])
            zs[i, hr:crows, :] = (
                qs[i, cy, cx, hr:crows, :].astype(f32) + r1y[i, cx].astype(f32)
                + r2x[i].astype(f32)
            ).astype(bf16)
            if i == 0:
                @pl.when(here)
                def _():
                    fin[cx] = zs[0]
            copy(
                zs.at[i], fin.at[cx], (2 * t + cy, level[i]), fs[0] + cx,
                when=away if i == 0 else None,
            )

        xt[:, mine] = x[mine, :].T
        arrive(xs, x.at[theirs])
        xt[:, theirs] = x[theirs, :].T
        weight_term(0)
        second_phase(0)
        send_gv()
        pass_on(3)
        pass_over(1)
        weight_term(1)
        pass_on(2)
        pass_over(3)
        weight_term(3)
        second_phase(1)
        pass_over(2)
        weight_term(2)
        second_phase(3)
        finish(1)
        second_phase(2)
        finish(3)
        finish(2)
        finish(0)
        loads[4].wait()
        for i in range(1, n):
            arrive(ws[i], wfull.at[level[i]])
        grad_in()
        arrive(vs, vals.at[mine])

    sent_g = list(pending)
    pending.clear()

    for h in range(heads):
        cols = slice(h * HD, (h + 1) * HD)
        grad_probs = lax.dot_general(
            ga[:, cols], vals[mine, cols], contract, preferred_element_type=f32
        )
        p = probs[h]
        row_dot = jnp.sum(p * grad_probs, axis=-1, keepdims=True)
        gs = (p * (grad_probs - row_dot) * scale).astype(bf16)
        gq[:, cols] = jnp.dot(gs, keys[:, cols], preferred_element_type=f32).astype(bf16)
        gk[:, cols] = lax.dot_general(
            gs, queries[:, cols], (((0,), (0,)), ((), ())), preferred_element_type=f32
        ).astype(bf16)

    groups = float(2 * chips)
    for j in range(chips // 2):
        local = jnp.logical_and(here, jnp.logical_and(k == 1, cx == j))

        @pl.when(jnp.logical_not(local))
        def _():
            arrive(fs[j], fin.at[j])
        gw[j * crows:(j + 1) * crows, :] = fin[j].astype(f32) / groups

    for role, sent in enumerate((sent_w, sent_g)):
        @pl.when(k == role)
        def _():
            drain(sent)
    assert counts[0] <= send_sem.shape[0] and counts[1] <= recv_sem.shape[0], counts


def write_out(*refs):
    results, outs, sem = refs[:4], refs[4:8], refs[8]
    moves = [
        pltpu.make_async_copy(results[i], outs[i], sem.at[i]) for i in range(4)
    ]
    for move in moves:
        move.start()
    for move in moves:
        move.wait()


def fused(n, groups, saved_input, queries, keys, value_weight, grad_attended):
    chips = groups // 2
    tokens, feat = saved_input.shape
    depth, width = value_weight.shape
    crows = feat // chips
    bf16 = jnp.bfloat16
    levels = n - 1
    vmem = pl.BlockSpec(memory_space=pltpu.VMEM)
    results = pl.pallas_call(
        functools.partial(fused_kernel, n, chips),
        out_shape=(
            pltpu.VMEM((tokens, feat), bf16),
            pltpu.VMEM((depth // groups, width), jnp.float32),
            pltpu.VMEM(queries.shape, bf16),
            pltpu.VMEM(keys.shape, bf16),
        ),
        in_specs=[pl.BlockSpec(memory_space=pl.ANY)] * 5,
        out_specs=(vmem,) * 4,
        scratch_shapes=[
            pltpu.VMEM((2 * tokens, feat), bf16),
            pltpu.VMEM(queries.shape, bf16),
            pltpu.VMEM(keys.shape, bf16),
            pltpu.VMEM(grad_attended.shape, bf16),
            pltpu.VMEM((n, feat, width), bf16),
            pltpu.VMEM((n, 2 * tokens, width), bf16),
            pltpu.VMEM((feat, 2 * tokens), bf16),
            pltpu.VMEM((n, 2, chips // 2, crows, width), bf16),
            pltpu.VMEM((n, 2, crows // 2, width), bf16),
            pltpu.VMEM((n, 2, crows // 2, width), bf16),
            pltpu.VMEM((n, 2, crows // 2, width), bf16),
            pltpu.VMEM((n, crows // 2, width), bf16),
            pltpu.VMEM((n, crows // 2, width), bf16),
            pltpu.VMEM((n, crows, width), bf16),
            pltpu.VMEM((chips // 2, crows, width), bf16),
            pltpu.VMEM((levels, 2 * tokens, width), jnp.float32),
            pltpu.VMEM((levels, 2 * tokens, width), bf16),
            pltpu.VMEM((n, 2 * tokens, width), bf16),
            pltpu.VMEM((2 * tokens, width), bf16),
            pltpu.VMEM((width // HD, tokens, tokens), jnp.float32),
            pltpu.VMEM((levels, crows, width), bf16),
            pltpu.SemaphoreType.DMA((96,)),
            pltpu.SemaphoreType.DMA((96,)),
            pltpu.SemaphoreType.DMA((8,)),
        ],
        compiler_params=pltpu.CompilerParams(
            collective_id=0, has_side_effects=True, vmem_limit_bytes=58 * 2**20
        ),
    )(saved_input, queries, keys, value_weight, grad_attended)
    return pl.pallas_call(
        write_out,
        out_shape=tuple(jax.ShapeDtypeStruct(r.shape, r.dtype) for r in results),
        in_specs=[vmem] * 4,
        out_specs=(pl.BlockSpec(memory_space=pl.ANY),) * 4,
        scratch_shapes=[pltpu.SemaphoreType.DMA((4,))],
        compiler_params=pltpu.CompilerParams(vmem_limit_bytes=8 * 2**20),
    )(*results)


def on_device(saved_input, queries, keys, value_weight, grad_attended):
    token_count = queries.shape[0]
    local_width = value_weight.shape[1]
    local_heads = local_width // HD
    score_scale = 1.0 / jnp.sqrt(jnp.float32(HD))
    full_input = lax.all_gather(saved_input, "tensor", axis=1, tiled=True)
    values = jnp.dot(full_input, value_weight, preferred_element_type=jnp.float32).astype(
        jnp.bfloat16
    )
    query_heads = queries.reshape(token_count, local_heads, HD)
    key_heads = keys.reshape(token_count, local_heads, HD)
    value_heads = values.reshape(token_count, local_heads, HD)
    grad_heads = grad_attended.reshape(token_count, local_heads, HD)
    scores = (
        jnp.einsum("qhd,khd->hqk", query_heads, key_heads, preferred_element_type=jnp.float32)
        * score_scale
    )
    positions = lax.iota(jnp.int32, token_count)
    causal = positions[:, None] >= positions[None, :]
    scores = jnp.where(causal[None], scores, -jnp.inf)
    row_max = jnp.max(scores, axis=-1, keepdims=True)
    weights_exp = jnp.exp(scores - row_max)
    attention = weights_exp / jnp.sum(weights_exp, axis=-1, keepdims=True)
    probs_half = attention.astype(jnp.bfloat16)
    grad_values = jnp.einsum(
        "hqk,qhd->khd", probs_half, grad_heads, preferred_element_type=jnp.float32
    ).astype(jnp.bfloat16)
    grad_probs = jnp.einsum(
        "qhd,khd->hqk", grad_heads, value_heads, preferred_element_type=jnp.float32
    )
    row_dot = jnp.sum(attention * grad_probs, axis=-1, keepdims=True)
    grad_scores = (attention * (grad_probs - row_dot) * score_scale).astype(jnp.bfloat16)
    grad_queries = jnp.einsum(
        "hqk,khd->qhd", grad_scores, key_heads, preferred_element_type=jnp.float32
    ).astype(jnp.bfloat16)
    grad_keys = jnp.einsum(
        "hqk,qhd->khd", grad_scores, query_heads, preferred_element_type=jnp.float32
    ).astype(jnp.bfloat16)
    value_flat = grad_values.reshape(token_count, local_width)
    data_groups = lax.axis_size("dp")
    partial_value = lax.dot_general(
        value_flat, value_weight, (((1,), (1,)), ((), ())), preferred_element_type=jnp.float32
    )
    grad_input = lax.psum_scatter(
        partial_value.astype(jnp.bfloat16), "tensor", scatter_dimension=1, tiled=True
    )
    partial_value = lax.dot_general(
        full_input, value_flat, (((0,), (0,)), ((), ())), preferred_element_type=jnp.float32
    )
    summed = lax.psum_scatter(
        partial_value.astype(jnp.bfloat16), "dp", scatter_dimension=0, tiled=True
    ).astype(jnp.float32)
    grad_value_weight = summed / jnp.float32(data_groups)
    return (
        grad_input,
        grad_value_weight,
        grad_queries.reshape(token_count, local_width),
        grad_keys.reshape(token_count, local_width),
    )


def solution(mesh):
    placed = (
        P("dp", "tensor"),
        P("dp", "tensor"),
        P("dp", "tensor"),
        P(None, "tensor"),
        P("dp", "tensor"),
    )
    levels, groups = mesh.shape["tensor"], mesh.shape["dp"]
    run = on_device
    if groups == 2 * levels and levels == 4:
        run = functools.partial(fused, levels, groups)
    return jax.shard_map(
        run,
        mesh=mesh,
        in_specs=placed,
        out_specs=(P("dp", "tensor"), P("dp", "tensor"), P("dp", "tensor"), P("dp", "tensor")),
        check_vma=False,
    )
```

time: 58 us -> 53.3 us (0.919)
  the two profiles are of different devices: /device:TPU:0 before, /device:TPU:4 now
where the time goes in v1:
time: 53.3 us; the launch traced here: 53.2 us
  Pallas kernels  52.5 us (98%)
  between operations  0.64 us (1%)
    pallas_call x1, Pallas kernels, fused(): pl.pallas_call(functools.partial(fused_kernel, n, chips), out_shape=(pltp...  51.3 us
    pallas_call x1, Pallas kernels, fused(): pl.pallas_call(write_out, out_shape=tuple((jax.ShapeDtypeStruct(r.shape,...  1.25 us

profile of v1, /device:TPU:4, one launch (start us, length us, event | category | flops | bytes accessed | tf_op | source)
XLA Modules:
  0.0 53.2 jit_solution(8814001942726295473)
XLA Ops:
  0.6 51.3 %shard_map.84 = (bf16[256,1536]{1,0:T(8,128)(2,1)S(1)}, f32[768,256]{1,0:T(8,128)S(1)}, bf16[256,256]{1,0:T(8,128)(2,1)S(1)}, bf16[256,256]{1,0:T(8,128)(2,1)S(1)}) custom-call(bf16[256,1536]{1,0:T(8,128)(2,1)} %x_hbm.1, bf16[256,256]{1,0:T(8,128)(2,1)} %q_hbm.1, bf16[256,256]{1,0:T(8,128)(2,1)} %k_hbm.1, bf16[6144,256]{1,0:T(8,128)(2,1)} %w.1, ...), custom_call_target="tpu_custom_call" | custom-call | tf_op jit(solution)/shard_map/pallas_call | solution.py:402
  51.9 1.3 %shard_map.85 = (bf16[256,1536]{1,0:T(8,128)(2,1)}, f32[768,256]{1,0:T(8,128)}, bf16[256,256]{1,0:T(8,128)(2,1)}, bf16[256,256]{1,0:T(8,128)(2,1)}) custom-call(bf16[256,1536]{1,0:T(8,128)(2,1)S(1)} %get-tuple-element.8.refs_0_, f32[768,256]{1,0:T(8,128)S(1)} %get-tuple-element.9.refs_1_, bf16[256,256]{1,0:T(8,128)(2,1)S(1)} %get-tuple-element.10.refs_2_, ...), custom_call_target="tpu_custom_call" | custom-call | tf_op jit(solution)/shard_map/pallas_call | solution.py:442

commit v2 on v1

v2 whole, which is shorter than its diff:
```python
import functools
import math

import jax
import jax.numpy as jnp
from jax import lax
from jax.experimental import pallas as pl
from jax.experimental.pallas import tpu as pltpu
from jax.sharding import PartitionSpec as P

HD = 128
END_WEIGHT = (
    ("W", 2), ("W", 3), ("W", 1), ("start", 0), ("sp", 2), ("sp", 1), ("on", 2), ("x", 0),
    ("sp", 3), ("end", 2), ("on", 3), ("vp", 2), ("end", 3), ("vp", 3), ("on", 1),
    ("end", 1), ("vp", 1), ("fin", 0),
)
MIDDLE_WEIGHT = (
    ("W", 1), ("W", 3), ("start", 0), ("W", 2), ("sp", 2), ("sp", 3), ("on", 2), ("sp", 1),
    ("on", 3), ("end", 2), ("on", 1), ("x", 0), ("end", 1), ("vp", 2), ("end", 3),
    ("vp", 1), ("vp", 3), ("cs", 3), ("fin", 0),
)
END_GRAD = (
    ("tk", 1), ("start", 0), ("twin", 0), ("x", 0), ("wt", 0), ("gvm", 0), ("gvt", 0),
    ("tk", 2), ("s2", 0), ("wt", 2), ("wt", 1), ("s2", 2), ("tk", 3), ("wt", 3), ("f", 2),
    ("s2", 1), ("s2", 3), ("f", 0), ("f", 3), ("f", 1), ("fin", 0),
)
MIDDLE_GRAD = (
    ("gvm", 0), ("start", 0), ("twin", 0), ("gvt", 0), ("x", 0), ("wt", 0), ("tk", 1),
    ("tk", 3), ("wt", 3), ("wt", 1), ("tk", 2), ("s2", 3), ("wt", 2), ("s2", 1), ("f", 3),
    ("s2", 0), ("s2", 2), ("f", 2), ("f", 0), ("f", 1), ("fin", 0),
)
JOINED = (3,)


def fused_kernel(
    n, chips,
    x_hbm, q_hbm, k_hbm, w, ga_hbm,
    gi, fin, gq, gk,
    x, queries, keys, ga,
    wfull, gvall, xt, qs, r1x, r1y, t2, r2x, r2y, zs,
    part, vsend, vrecv, vsum, probs, wsend,
    send_sem, recv_sem, load_sem,
):
    f32, bf16 = jnp.float32, jnp.bfloat16
    tokens, width = queries.shape
    feat = x.shape[1]
    crows = feat // chips
    hr = crows // 2
    heads = width // HD
    t = lax.axis_index("tensor")
    d = lax.axis_index("dp")
    c, k = d // 2, d % 2
    cx, cy = c % 2, c // 2
    scale = 1.0 / (HD ** 0.5)
    last = n - 1
    upper = t // (n // 2)
    edge = (t % last) == 0
    mid = (t % last) != 0
    level = [t, t + 1 - 2 * (t % 2), last - last * upper, n // 2 - upper]

    def at(s):
        return (d, s)

    partner = (d + 1 - 2 * k, t)
    xn = (d + 2 - 4 * cx, t)
    yn = (d + 4 - 8 * cy, t)
    diagonal = (d + 2 - 4 * cx + 4 - 8 * cy, t)
    chip_x, chip_y, chip_d = c + 1 - 2 * cx, c + 2 - 4 * cy, last - c

    counts = [0, 0]
    sent = {}
    now = [None]

    def slot():
        counts[1] += 1
        return counts[1] - 1

    def slots():
        return [slot() for _ in range(n)]

    def copy(src, dst, device, recv):
        i = counts[0]
        counts[0] += 1
        cp = pltpu.make_async_remote_copy(
            src_ref=src, dst_ref=dst, send_sem=send_sem.at[i], recv_sem=recv_sem.at[recv],
            device_id=device, device_id_type=pl.DeviceIdType.MESH,
        )
        cp.start()
        sent.setdefault(now[0], []).append((i, math.prod(src.shape) * src.dtype.itemsize // (2 * width)))

    def drain(name):
        for i, size in sent[name]:
            ref = wfull.at[0, 0:size]
            pltpu.make_async_remote_copy(
                src_ref=ref, dst_ref=ref, send_sem=send_sem.at[i], recv_sem=recv_sem.at[0],
                device_id=partner, device_id_type=pl.DeviceIdType.MESH,
            ).wait_send()

    def arrive(recv, ref):
        pltpu.make_async_remote_copy(
            src_ref=ref, dst_ref=ref, send_sem=send_sem.at[0], recv_sem=recv_sem.at[recv],
            device_id=partner, device_id_type=pl.DeviceIdType.MESH,
        ).wait_recv()

    def rows(i, size):
        return pl.ds(pl.multiple_of(i * size, size), size)

    mine, theirs = rows(k, tokens), rows(1 - k, tokens)

    barrier = pltpu.get_barrier_semaphore()
    peers = [at((t + o) % n) for o in range(1, n)] + [xn, yn, diagonal, partner]
    for peer in peers:
        pl.semaphore_signal(
            barrier, inc=1, device_id=peer, device_id_type=pl.DeviceIdType.MESH
        )
    ahead = [
        pltpu.make_async_copy(
            w.at[pl.ds(pl.multiple_of(level[i] * feat + c * crows, crows), crows)],
            wsend.at[i - 1], load_sem.at[4 + i],
        )
        for i in range(1, n)
    ]
    loads = [
        pltpu.make_async_copy(src, dst, load_sem.at[i])
        for i, (src, dst) in enumerate([
            (q_hbm, queries), (k_hbm, keys), (ga_hbm, ga), (x_hbm, x.at[mine]),
            (w.at[rows(t, feat)], wfull.at[t]),
        ])
    ]

    @pl.when(k == 0)
    def _():
        for load in ahead:
            load.start()
    for load in loads[:4]:
        load.start()

    def attend():
        for load in loads[:3]:
            load.wait()
        row = lax.broadcasted_iota(jnp.int32, (tokens, tokens), 0)
        col = lax.broadcasted_iota(jnp.int32, (tokens, tokens), 1)
        causal = row >= col
        for h in range(heads):
            cols = slice(h * HD, (h + 1) * HD)
            scores = lax.dot_general(
                queries[:, cols], keys[:, cols], (((1,), (1,)), ((), ())),
                preferred_element_type=f32,
            ) * scale
            scores = jnp.where(causal, scores, -jnp.inf)
            e = jnp.exp(scores - jnp.max(scores, axis=-1, keepdims=True))
            p = e / jnp.sum(e, axis=-1, keepdims=True)
            probs[h] = p
            gvall[t, mine, cols] = lax.dot_general(
                p.astype(bf16), ga[:, cols], (((0,), (0,)), ((), ())),
                preferred_element_type=f32,
            ).astype(bf16)
        loads[3].wait()
        loads[4].start()

    def everyone():
        pl.semaphore_wait(barrier, len(peers))

    xs, gvs, ws, vs = slot(), slots(), slots(), slot()
    gza, gzb = slots(), slots()
    wz, wpx, wpy, wqx, wqy, wrx, wry = (slots() for _ in range(7))
    p1x, p1y, p2x, p2y = slots(), slots(), slots(), slots()
    vz, pc = slots(), slots()
    fs = [slot() for _ in range(chips // 2)]
    home = c == t
    here = jnp.logical_and(home, cy == 1)
    away = jnp.logical_not(here)
    contract = (((1,), (1,)), ((), ()))

    def grad_in():
        acc = lax.dot_general(
            gvall[t, mine, :], wfull[t], contract, preferred_element_type=f32
        )
        for i in range(1, n):
            acc = acc + lax.dot_general(
                gvall[level[i], mine, :], wfull[level[i]], contract,
                preferred_element_type=f32,
            )
        gi[...] = acc.astype(bf16)

    def chunk(i, who, first=0, size=crows):
        start = pl.multiple_of(who * crows, crows) + first
        return wfull.at[level[i], pl.ds(pl.multiple_of(start, hr), size)]

    def weight_chain(end):
        for load in ahead:
            load.wait()
        everyone()

        def send_weight(i):
            copy(
                wsend.at[i - 1],
                wfull.at[t, rows(c, crows)],
                at(level[i]),
                wz[1] if i == 1 else wz[2] if end else wz[3],
            )

        def start(_):
            attend()
            copy(gvall.at[t, mine], gvall.at[t, mine], partner, gvs[0])
            copy(x.at[mine], x.at[mine], partner, xs)

        def spread(i):
            arrive(wz[i], chunk(i, c))
            low, high = chunk(i, c, 0, hr), chunk(i, c, hr, hr)
            copy(high, high, xn, wpx[i])
            copy(low, low, yn, wpy[i])
            copy(low, low, xn, wqx[i])
            copy(high, high, yn, wqy[i])

        def spread_on(i):
            piece = chunk(i, chip_x, hr, hr)
            arrive(wpx[i], piece)
            copy(piece, piece, yn, wry[i])
            piece = chunk(i, chip_y, 0, hr)
            arrive(wpy[i], piece)
            copy(piece, piece, xn, wrx[i])

        def spread_end(i):
            arrive(wqx[i], chunk(i, chip_x, 0, hr))
            arrive(wqy[i], chunk(i, chip_y, hr, hr))
            arrive(wrx[i], chunk(i, chip_d, 0, hr))
            arrive(wry[i], chunk(i, chip_d, hr, hr))
            copy(wfull.at[level[i]], wfull.at[level[i]], partner, ws[i])

        def value_send(i, seen):
            for j in range(2):
                copy(
                    vsend.at[i - 1, rows(j, tokens)], vrecv.at[seen - 1],
                    (2 * c + j, level[i]), vz[seen],
                )

        def value_part(i):
            vsend[i - 1] = jnp.dot(
                x[...], wfull[level[i]], preferred_element_type=f32
            ).astype(bf16)
            if i not in JOINED:
                value_send(i, 1 if i == 1 else 2 if end else 3)
            elif end:
                copy(vsend.at[i - 1], vsum.at[i - 2], at(level[1]), pc[i])

        def value_join(i):
            arrive(pc[i], vsum.at[i - 2])
            vsend[i - 1] = (vsend[i - 1].astype(f32) + vsum[i - 2].astype(f32)).astype(bf16)
            value_send(i, 3)

        def close(_):
            loads[4].wait()
            own = jnp.dot(x[...], wfull[t], preferred_element_type=f32)
            part[0] = own[0:tokens]
            part[1] = own[tokens:2 * tokens]
            copy(part.at[1], part.at[0], partner, vs)
            for i in range(1, n):
                arrive(gvs[i], gvall.at[glevel(end, i), mine])
            grad_in()
            gather(end)

        steps = {
            "W": send_weight, "start": start, "sp": spread, "on": spread_on,
            "end": spread_end, "vp": value_part, "cs": value_join, "fin": close,
            "x": lambda _: arrive(xs, x.at[theirs]),
        }
        for op, i in END_WEIGHT if end else MIDDLE_WEIGHT:
            steps[op](i)

    def gather(end):
        total = part[0]
        for i in range(1, n):
            if i != 2 or (2 if end else 3) not in JOINED:
                arrive(vz[i], vrecv.at[i - 1])
                total = total + vrecv[i - 1].astype(f32)
        part[0] = total

    def glevel(end, i):
        return level[(0, 1, 3, 2)[i] if end else (0, 3, 1, 2)[i]]

    def grad_chain(end):
        def gv(i, which):
            return gvall.at[glevel(end, i), which]

        def send_gv(which, sem):
            for to, got in ((1, 2), (3, 3)) if end else ((3, 1), (1, 1)):
                copy(gv(0, which), gv(0, which), at(level[to]), sem[got])

        attend()
        everyone()
        def start(_):
            copy(x.at[mine], x.at[mine], partner, xs)

        def turn(_):
            xt[:, mine] = x[mine, :].T
            arrive(xs, x.at[theirs])
            xt[:, theirs] = x[theirs, :].T

        def take(i):
            for which, sem in ((mine, gza), (theirs, gzb)):
                arrive(sem[i], gv(i, which))
                if not end and i != 2:
                    copy(gv(i, which), gv(i, which), at(level[1]), sem[(2, 2, 2, 3)[i]])
            copy(gv(i, theirs), gv(i, theirs), partner, gvs[i])

        def weight_term(i):
            term = jnp.dot(
                xt[...], gvall[glevel(end, i)], preferred_element_type=f32
            ).astype(bf16)
            for j in range(chips):
                qs[i, j // 2, j % 2] = term[j * crows:(j + 1) * crows]
            copy(qs.at[i, :, 1 - cx, 0:hr, :], r1x.at[i], xn, p1x[i])
            copy(qs.at[i, 1 - cy, :, hr:crows, :], r1y.at[i], yn, p1y[i])

        def second_phase(i):
            arrive(p1x[i], r1x.at[i])
            t2[i, 0] = (
                qs[i, 1 - cy, cx, 0:hr, :].astype(f32) + r1x[i, 1 - cy].astype(f32)
            ).astype(bf16)
            copy(t2.at[i, 0], r2y.at[i], yn, p2y[i])
            arrive(p1y[i], r1y.at[i])
            t2[i, 1] = (
                qs[i, cy, 1 - cx, hr:crows, :].astype(f32) + r1y[i, 1 - cx].astype(f32)
            ).astype(bf16)
            copy(t2.at[i, 1], r2x.at[i], xn, p2x[i])

        def finish(i):
            arrive(p2y[i], r2y.at[i])
            zs[i, 0:hr, :] = (
                qs[i, cy, cx, 0:hr, :].astype(f32) + r1x[i, cy].astype(f32)
                + r2y[i].astype(f32)
            ).astype(bf16)
            arrive(p2x[i], r2x.at[i])
            zs[i, hr:crows, :] = (
                qs[i, cy, cx, hr:crows, :].astype(f32) + r1y[i, cx].astype(f32)
                + r2x[i].astype(f32)
            ).astype(bf16)
            if i > 0:
                copy(zs.at[i], fin.at[cx], (2 * t + cy, glevel(end, i)), fs[0] + cx)
            else:
                @pl.when(here)
                def _():
                    fin[cx] = zs[0]

                @pl.when(away)
                def _():
                    own_final().start()

        def close(_):
            loads[4].wait()
            for i in range(1, n):
                arrive(ws[i], wfull.at[level[i]])
            grad_in()
            arrive(vs, part.at[0])
            gather(end)

        steps = {
            "start": start, "x": turn, "tk": take, "wt": weight_term, "s2": second_phase,
            "f": finish, "fin": close,
            "twin": lambda _: arrive(gvs[0], gv(0, theirs)),
            "gvm": lambda _: send_gv(mine, gza),
            "gvt": lambda _: send_gv(theirs, gzb),
        }
        for op, i in END_GRAD if end else MIDDLE_GRAD:
            steps[op](i)

    def own_final():
        return pltpu.make_async_remote_copy(
            src_ref=zs.at[0], dst_ref=fin.at[cx],
            send_sem=send_sem.at[send_sem.shape[0] - 1], recv_sem=recv_sem.at[fs[0] + cx],
            device_id=(2 * t + cy, t), device_id_type=pl.DeviceIdType.MESH,
        )

    for role, chain in enumerate((weight_chain, grad_chain)):
        for end in (True, False):
            now[0] = (role, end)

            @pl.when(jnp.logical_and(k == role, edge if end else mid))
            def _():
                chain(end)

    values = part[0].astype(bf16)
    for h in range(heads):
        cols = slice(h * HD, (h + 1) * HD)
        grad_probs = lax.dot_general(
            ga[:, cols], values[:, cols], contract, preferred_element_type=f32
        )
        p = probs[h]
        row_dot = jnp.sum(p * grad_probs, axis=-1, keepdims=True)
        gs = (p * (grad_probs - row_dot) * scale).astype(bf16)
        gq[:, cols] = jnp.dot(gs, keys[:, cols], preferred_element_type=f32).astype(bf16)
        gk[:, cols] = lax.dot_general(
            gs, queries[:, cols], (((0,), (0,)), ((), ())), preferred_element_type=f32
        ).astype(bf16)

    for j in range(chips // 2):
        local = jnp.logical_and(here, jnp.logical_and(k == 1, cx == j))

        @pl.when(jnp.logical_not(local))
        def _():
            arrive(fs[j], fin.at[j])

    @pl.when(jnp.logical_and(k == 1, away))
    def _():
        own_final().wait_send()

    for role in range(2):
        for end in (True, False):
            @pl.when(jnp.logical_and(k == role, edge if end else mid))
            def _():
                drain((role, end))
    assert counts[0] < send_sem.shape[0] and counts[1] <= recv_sem.shape[0], counts


def write_out(groups, gi_in, fin, gq_in, gk_in, gi, gw, gq, gk, part, sem):
    crows = fin.shape[1]
    moves = []

    def move(src, dst):
        cp = pltpu.make_async_copy(src, dst, sem.at[len(moves)])
        cp.start()
        moves.append(cp)

    move(gi_in, gi)
    move(gq_in, gq)
    move(gk_in, gk)
    for j in range(fin.shape[0]):
        part[j] = fin[j].astype(jnp.float32) / groups
        move(part.at[j], gw.at[pl.ds(j * crows, crows)])
    for cp in moves:
        cp.wait()


def fused(n, groups, saved_input, queries, keys, value_weight, grad_attended):
    chips = groups // 2
    tokens, feat = saved_input.shape
    depth, width = value_weight.shape
    crows = feat // chips
    bf16 = jnp.bfloat16
    levels = n - 1
    vmem = pl.BlockSpec(memory_space=pltpu.VMEM)
    results = pl.pallas_call(
        functools.partial(fused_kernel, n, chips),
        out_shape=(
            pltpu.VMEM((tokens, feat), bf16),
            pltpu.VMEM((chips // 2, crows, width), bf16),
            pltpu.VMEM(queries.shape, bf16),
            pltpu.VMEM(keys.shape, bf16),
        ),
        in_specs=[pl.BlockSpec(memory_space=pl.ANY)] * 5,
        out_specs=(vmem,) * 4,
        scratch_shapes=[
            pltpu.VMEM((2 * tokens, feat), bf16),
            pltpu.VMEM(queries.shape, bf16),
            pltpu.VMEM(keys.shape, bf16),
            pltpu.VMEM(grad_attended.shape, bf16),
            pltpu.VMEM((n, feat, width), bf16),
            pltpu.VMEM((n, 2 * tokens, width), bf16),
            pltpu.VMEM((feat, 2 * tokens), bf16),
            pltpu.VMEM((n, 2, chips // 2, crows, width), bf16),
            pltpu.VMEM((n, 2, crows // 2, width), bf16),
            pltpu.VMEM((n, 2, crows // 2, width), bf16),
            pltpu.VMEM((n, 2, crows // 2, width), bf16),
            pltpu.VMEM((n, crows // 2, width), bf16),
            pltpu.VMEM((n, crows // 2, width), bf16),
            pltpu.VMEM((n, crows, width), bf16),
            pltpu.VMEM((2, tokens, width), jnp.float32),
            pltpu.VMEM((levels, 2 * tokens, width), bf16),
            pltpu.VMEM((levels, tokens, width), bf16),
            pltpu.VMEM((2, 2 * tokens, width), bf16),
            pltpu.VMEM((width // HD, tokens, tokens), jnp.float32),
            pltpu.VMEM((levels, crows, width), bf16),
            pltpu.SemaphoreType.DMA((160,)),
            pltpu.SemaphoreType.DMA((96,)),
            pltpu.SemaphoreType.DMA((8,)),
        ],
        compiler_params=pltpu.CompilerParams(
            collective_id=0, has_side_effects=True, vmem_limit_bytes=58 * 2**20
        ),
    )(saved_input, queries, keys, value_weight, grad_attended)
    outs = (
        (saved_input.shape, bf16), ((depth // groups, width), jnp.float32),
        (queries.shape, bf16), (keys.shape, bf16),
    )
    return pl.pallas_call(
        functools.partial(write_out, float(groups)),
        out_shape=tuple(jax.ShapeDtypeStruct(*out) for out in outs),
        in_specs=[vmem] * 4,
        out_specs=(pl.BlockSpec(memory_space=pl.ANY),) * 4,
        scratch_shapes=[
            pltpu.VMEM((chips // 2, crows, width), jnp.float32),
            pltpu.SemaphoreType.DMA((3 + chips // 2,)),
        ],
        compiler_params=pltpu.CompilerParams(vmem_limit_bytes=8 * 2**20),
    )(*results)


def on_device(saved_input, queries, keys, value_weight, grad_attended):
    token_count = queries.shape[0]
    local_width = value_weight.shape[1]
    local_heads = local_width // HD
    score_scale = 1.0 / jnp.sqrt(jnp.float32(HD))
    full_input = lax.all_gather(saved_input, "tensor", axis=1, tiled=True)
    values = jnp.dot(full_input, value_weight, preferred_element_type=jnp.float32).astype(
        jnp.bfloat16
    )
    query_heads = queries.reshape(token_count, local_heads, HD)
    key_heads = keys.reshape(token_count, local_heads, HD)
    value_heads = values.reshape(token_count, local_heads, HD)
    grad_heads = grad_attended.reshape(token_count, local_heads, HD)
    scores = (
        jnp.einsum("qhd,khd->hqk", query_heads, key_heads, preferred_element_type=jnp.float32)
        * score_scale
    )
    positions = lax.iota(jnp.int32, token_count)
    causal = positions[:, None] >= positions[None, :]
    scores = jnp.where(causal[None], scores, -jnp.inf)
    row_max = jnp.max(scores, axis=-1, keepdims=True)
    weights_exp = jnp.exp(scores - row_max)
    attention = weights_exp / jnp.sum(weights_exp, axis=-1, keepdims=True)
    probs_half = attention.astype(jnp.bfloat16)
    grad_values = jnp.einsum(
        "hqk,qhd->khd", probs_half, grad_heads, preferred_element_type=jnp.float32
    ).astype(jnp.bfloat16)
    grad_probs = jnp.einsum(
        "qhd,khd->hqk", grad_heads, value_heads, preferred_element_type=jnp.float32
    )
    row_dot = jnp.sum(attention * grad_probs, axis=-1, keepdims=True)
    grad_scores = (attention * (grad_probs - row_dot) * score_scale).astype(jnp.bfloat16)
    grad_queries = jnp.einsum(
        "hqk,khd->qhd", grad_scores, key_heads, preferred_element_type=jnp.float32
    ).astype(jnp.bfloat16)
    grad_keys = jnp.einsum(
        "hqk,qhd->khd", grad_scores, query_heads, preferred_element_type=jnp.float32
    ).astype(jnp.bfloat16)
    value_flat = grad_values.reshape(token_count, local_width)
    data_groups = lax.axis_size("dp")
    partial_value = lax.dot_general(
        value_flat, value_weight, (((1,), (1,)), ((), ())), preferred_element_type=jnp.float32
    )
    grad_input = lax.psum_scatter(
        partial_value.astype(jnp.bfloat16), "tensor", scatter_dimension=1, tiled=True
    )
    partial_value = lax.dot_general(
        full_input, value_flat, (((0,), (0,)), ((), ())), preferred_element_type=jnp.float32
    )
    summed = lax.psum_scatter(
        partial_value.astype(jnp.bfloat16), "dp", scatter_dimension=0, tiled=True
    ).astype(jnp.float32)
    grad_value_weight = summed / jnp.float32(data_groups)
    return (
        grad_input,
        grad_value_weight,
        grad_queries.reshape(token_count, local_width),
        grad_keys.reshape(token_count, local_width),
    )


def solution(mesh):
    placed = (
        P("dp", "tensor"),
        P("dp", "tensor"),
        P("dp", "tensor"),
        P(None, "tensor"),
        P("dp", "tensor"),
    )
    levels, groups = mesh.shape["tensor"], mesh.shape["dp"]
    run = on_device
    if groups == 2 * levels and levels == 4:
        run = functools.partial(fused, levels, groups)
    return jax.shard_map(
        run,
        mesh=mesh,
        in_specs=placed,
        out_specs=(P("dp", "tensor"), P("dp", "tensor"), P("dp", "tensor"), P("dp", "tensor")),
        check_vma=False,
    )
```

time: 53.3 us -> 49.7 us (0.932)
  the two profiles are of different devices: /device:TPU:4 before, /device:TPU:3 now
where the time goes in v2:
time: 49.7 us; the launch traced here: 49 us
  Pallas kernels  48.2 us (97%)
  between operations  0.82 us (2%)
    pallas_call x1, Pallas kernels, fused(): pl.pallas_call(functools.partial(fused_kernel, n, chips), out_shape=(pltp...  46.9 us
    pallas_call x1, Pallas kernels, fused(): pl.pallas_call(functools.partial(write_out, float(groups)), out_shape=tup...  1.27 us

profile of v2, /device:TPU:3, one launch (start us, length us, event | category | flops | bytes accessed | tf_op | source)
XLA Modules:
  0.0 49.0 jit_solution(3507220727836210631)
XLA Ops:
  0.6 46.9 %shard_map.84 = (bf16[256,1536]{1,0:T(8,128)(2,1)S(1)}, bf16[2,384,256]{2,1,0:T(8,128)(2,1)S(1)}, bf16[256,256]{1,0:T(8,128)(2,1)S(1)}, bf16[256,256]{1,0:T(8,128)(2,1)S(1)}) custom-call(bf16[256,1536]{1,0:T(8,128)(2,1)} %x_hbm.1, bf16[256,256]{1,0:T(8,128)(2,1)} %q_hbm.1, bf16[256,256]{1,0:T(8,128)(2,1)} %k_hbm.1, bf16[6144,256]{1,0:T(8,128)(2,1)} %w.1, ...), custom_call_target="tpu_custom_call" | custom-call | tf_op jit(solution)/shard_map/pallas_call | solution.py:443
  47.6 1.3 %shard_map.85 = (bf16[256,1536]{1,0:T(8,128)(2,1)}, f32[768,256]{1,0:T(8,128)}, bf16[256,256]{1,0:T(8,128)(2,1)}, bf16[256,256]{1,0:T(8,128)(2,1)}) custom-call(bf16[256,1536]{1,0:T(8,128)(2,1)S(1)} %get-tuple-element.8.gi_in, bf16[2,384,256]{2,1,0:T(8,128)(2,1)S(1)} %get-tuple-element.9.fin, bf16[256,256]{1,0:T(8,128)(2,1)S(1)} %get-tuple-element.10.gq_in, ...), custom_call_target="tpu_custom_call" | custom-call | tf_op jit(solution)/shard_map/pallas_call | solution.py:486

commit v3 on v2

--- a/solution.py
+++ b/solution.py
@@ -22,12 +22,12 @@
 END_GRAD = (
     ("tk", 1), ("start", 0), ("twin", 0), ("x", 0), ("wt", 0), ("gvm", 0), ("gvt", 0),
     ("tk", 2), ("s2", 0), ("wt", 2), ("wt", 1), ("s2", 2), ("tk", 3), ("wt", 3), ("f", 2),
-    ("s2", 1), ("s2", 3), ("f", 0), ("f", 3), ("f", 1), ("fin", 0),
+    ("s2", 3), ("s2", 1), ("f", 0), ("f", 3), ("f", 1), ("fin", 0),
 )
 MIDDLE_GRAD = (
     ("gvm", 0), ("start", 0), ("twin", 0), ("gvt", 0), ("x", 0), ("wt", 0), ("tk", 1),
     ("tk", 3), ("wt", 3), ("wt", 1), ("tk", 2), ("s2", 3), ("wt", 2), ("s2", 1), ("f", 3),
-    ("s2", 0), ("s2", 2), ("f", 2), ("f", 0), ("f", 1), ("fin", 0),
+    ("s2", 0), ("s2", 2), ("f", 0), ("f", 1), ("f", 2), ("fin", 0),
 )
 JOINED = (3,)
 
@@ -166,7 +166,7 @@
     wz, wpx, wpy, wqx, wqy, wrx, wry = (slots() for _ in range(7))
     p1x, p1y, p2x, p2y = slots(), slots(), slots(), slots()
     vz, pc = slots(), slots()
-    fs = [slot() for _ in range(chips // 2)]
+    fs = [[slot() for _ in range(chips // 2)] for _ in range(2)]
     home = c == t
     here = jnp.logical_and(home, cy == 1)
     away = jnp.logical_not(here)
@@ -326,26 +326,28 @@
             copy(t2.at[i, 1], r2x.at[i], xn, p2x[i])
 
         def finish(i):
-            arrive(p2y[i], r2y.at[i])
-            zs[i, 0:hr, :] = (
-                qs[i, cy, cx, 0:hr, :].astype(f32) + r1x[i, cy].astype(f32)
-                + r2y[i].astype(f32)
-            ).astype(bf16)
-            arrive(p2x[i], r2x.at[i])
-            zs[i, hr:crows, :] = (
-                qs[i, cy, cx, hr:crows, :].astype(f32) + r1y[i, cx].astype(f32)
-                + r2x[i].astype(f32)
-            ).astype(bf16)
-            if i > 0:
-                copy(zs.at[i], fin.at[cx], (2 * t + cy, glevel(end, i)), fs[0] + cx)
-            else:
-                @pl.when(here)
-                def _():
-                    fin[cx] = zs[0]
-
-                @pl.when(away)
-                def _():
-                    own_final().start()
+            for j, (mine_in, first, second) in enumerate((
+                (p2y[i], r1x[i, cy], r2y), (p2x[i], r1y[i, cx], r2x),
+            )):
+                part_rows = slice(j * hr, (j + 1) * hr)
+                arrive(mine_in, second.at[i])
+                zs[i, part_rows, :] = (
+                    qs[i, cy, cx, part_rows, :].astype(f32) + first.astype(f32)
+                    + second[i].astype(f32)
+                ).astype(bf16)
+                if i > 0:
+                    copy(
+                        zs.at[i, part_rows], fin.at[cx, part_rows],
+                        (2 * t + cy, glevel(end, i)), fs[j][0] + cx,
+                    )
+                else:
+                    @pl.when(here)
+                    def _():
+                        fin[cx, part_rows] = zs[0, part_rows]
+
+                    @pl.when(away)
+                    def _():
+                        own_final(j).start()
 
         def close(_):
             loads[4].wait()
@@ -365,10 +367,12 @@
         for op, i in END_GRAD if end else MIDDLE_GRAD:
             steps[op](i)
 
-    def own_final():
+    def own_final(j):
+        part_rows = slice(j * hr, (j + 1) * hr)
         return pltpu.make_async_remote_copy(
-            src_ref=zs.at[0], dst_ref=fin.at[cx],
-            send_sem=send_sem.at[send_sem.shape[0] - 1], recv_sem=recv_sem.at[fs[0] + cx],
+            src_ref=zs.at[0, part_rows], dst_ref=fin.at[cx, part_rows],
+            send_sem=send_sem.at[send_sem.shape[0] - 1 - j],
+            recv_sem=recv_sem.at[fs[j][0] + cx],
             device_id=(2 * t + cy, t), device_id_type=pl.DeviceIdType.MESH,
         )
 
@@ -399,18 +403,20 @@
 
         @pl.when(jnp.logical_not(local))
         def _():
-            arrive(fs[j], fin.at[j])
+            for h in range(2):
+                arrive(fs[h][j], fin.at[j, h * hr:(h + 1) * hr])
 
     @pl.when(jnp.logical_and(k == 1, away))
     def _():
-        own_final().wait_send()
+        for j in range(2):
+            own_final(j).wait_send()
 
     for role in range(2):
         for end in (True, False):
             @pl.when(jnp.logical_and(k == role, edge if end else mid))
             def _():
                 drain((role, end))
-    assert counts[0] < send_sem.shape[0] and counts[1] <= recv_sem.shape[0], counts
+    assert counts[0] < send_sem.shape[0] - 1 and counts[1] <= recv_sem.shape[0], counts
 
 
 def write_out(groups, gi_in, fin, gq_in, gk_in, gi, gw, gq, gk, part, sem):
@@ -471,7 +477,7 @@
             pltpu.VMEM((2, 2 * tokens, width), bf16),
             pltpu.VMEM((width // HD, tokens, tokens), jnp.float32),
             pltpu.VMEM((levels, crows, width), bf16),
-            pltpu.SemaphoreType.DMA((160,)),
+            pltpu.SemaphoreType.DMA((192,)),
             pltpu.SemaphoreType.DMA((96,)),
             pltpu.SemaphoreType.DMA((8,)),
         ],

time: 49.7 us -> 49.5 us (level); the launches traced: 49 us -> 49.4 us
  no operation moved by 1% of the time
where the time goes in v3:
time: 49.5 us; the launch traced here: 49.4 us
  Pallas kernels  48.5 us (98%)
  between operations  0.82 us (2%)
    pallas_call x1, Pallas kernels, fused(): pl.pallas_call(functools.partial(fused_kernel, n, chips), out_shape=(pltp...  47.3 us
    pallas_call x1, Pallas kernels, fused(): pl.pallas_call(functools.partial(write_out, float(groups)), out_shape=tup...  1.27 us

profile of v3, /device:TPU:3, one launch (start us, length us, event | category | flops | bytes accessed | tf_op | source)
XLA Modules:
  0.0 49.4 jit_solution(12806813582207949996)
XLA Ops:
  0.6 47.3 %shard_map.84 = (bf16[256,1536]{1,0:T(8,128)(2,1)S(1)}, bf16[2,384,256]{2,1,0:T(8,128)(2,1)S(1)}, bf16[256,256]{1,0:T(8,128)(2,1)S(1)}, bf16[256,256]{1,0:T(8,128)(2,1)S(1)}) custom-call(bf16[256,1536]{1,0:T(8,128)(2,1)} %x_hbm.1, bf16[256,256]{1,0:T(8,128)(2,1)} %q_hbm.1, bf16[256,256]{1,0:T(8,128)(2,1)} %k_hbm.1, bf16[6144,256]{1,0:T(8,128)(2,1)} %w.1, ...), custom_call_target="tpu_custom_call" | custom-call | tf_op jit(solution)/shard_map/pallas_call | solution.py:449
  47.9 1.3 %shard_map.85 = (bf16[256,1536]{1,0:T(8,128)(2,1)}, f32[768,256]{1,0:T(8,128)}, bf16[256,256]{1,0:T(8,128)(2,1)}, bf16[256,256]{1,0:T(8,128)(2,1)}) custom-call(bf16[256,1536]{1,0:T(8,128)(2,1)S(1)} %get-tuple-element.8.gi_in, bf16[2,384,256]{2,1,0:T(8,128)(2,1)S(1)} %get-tuple-element.9.fin, bf16[256,256]{1,0:T(8,128)(2,1)S(1)} %get-tuple-element.10.gq_in, ...), custom_call_target="tpu_custom_call" | custom-call | tf_op jit(solution)/shard_map/pallas_call | solution.py:492

commit v4 on v3

--- a/solution.py
+++ b/solution.py
@@ -20,7 +20,7 @@
     ("vp", 1), ("vp", 3), ("cs", 3), ("fin", 0),
 )
 END_GRAD = (
-    ("tk", 1), ("start", 0), ("twin", 0), ("x", 0), ("wt", 0), ("gvm", 0), ("gvt", 0),
+    ("start", 0), ("twin", 0), ("tk", 1), ("x", 0), ("wt", 0), ("gvm", 0), ("gvt", 0),
     ("tk", 2), ("s2", 0), ("wt", 2), ("wt", 1), ("s2", 2), ("tk", 3), ("wt", 3), ("f", 2),
     ("s2", 3), ("s2", 1), ("f", 0), ("f", 3), ("f", 1), ("fin", 0),
 )

time: 49.5 us -> 49.5 us (level)
  no operation moved by 1% of the time
where the time goes in v4:
time: 49.5 us; the launch traced here: 49.4 us
  Pallas kernels  48.5 us (98%)
  between operations  0.82 us (2%)
    pallas_call x1, Pallas kernels, fused(): pl.pallas_call(functools.partial(fused_kernel, n, chips), out_shape=(pltp...  47.3 us
    pallas_call x1, Pallas kernels, fused(): pl.pallas_call(functools.partial(write_out, float(groups)), out_shape=tup...  1.27 us

profile of v4, /device:TPU:3, one launch (start us, length us, event | category | flops | bytes accessed | tf_op | source)
XLA Modules:
  0.0 49.4 jit_solution(1207573310764242398)
XLA Ops:
  0.6 47.3 %shard_map.84 = (bf16[256,1536]{1,0:T(8,128)(2,1)S(1)}, bf16[2,384,256]{2,1,0:T(8,128)(2,1)S(1)}, bf16[256,256]{1,0:T(8,128)(2,1)S(1)}, bf16[256,256]{1,0:T(8,128)(2,1)S(1)}) custom-call(bf16[256,1536]{1,0:T(8,128)(2,1)} %x_hbm.1, bf16[256,256]{1,0:T(8,128)(2,1)} %q_hbm.1, bf16[256,256]{1,0:T(8,128)(2,1)} %k_hbm.1, bf16[6144,256]{1,0:T(8,128)(2,1)} %w.1, ...), custom_call_target="tpu_custom_call" | custom-call | tf_op jit(solution)/shard_map/pallas_call | solution.py:449
  47.9 1.3 %shard_map.85 = (bf16[256,1536]{1,0:T(8,128)(2,1)}, f32[768,256]{1,0:T(8,128)}, bf16[256,256]{1,0:T(8,128)(2,1)}, bf16[256,256]{1,0:T(8,128)(2,1)}) custom-call(bf16[256,1536]{1,0:T(8,128)(2,1)S(1)} %get-tuple-element.8.gi_in, bf16[2,384,256]{2,1,0:T(8,128)(2,1)S(1)} %get-tuple-element.9.fin, bf16[256,256]{1,0:T(8,128)(2,1)S(1)} %get-tuple-element.10.gq_in, ...), custom_call_target="tpu_custom_call" | custom-call | tf_op jit(solution)/shard_map/pallas_call | solution.py:492
